TPU v7x, 32 devices: a whole 2x2x4 slice. The times are simulated.
32 devices in a mesh: kv: 2 (over core), seq: 16 (over z, y, x), dp: 1.
Axes of the slice: x: 2, y: 2, z: 4, core: 2. Of those that a mesh axis runs over, the one named last changes fastest.
Arguments:
- token_input_state: bfloat16 [4, 8192], P('dp'), may hold values from -6 to 6
- query_matrix: bfloat16 [8192, 2048], P('seq', 'kv'), may hold values from -0.0625 to 0.0625
- key_value_weight: bfloat16 [8192, 512], P('seq', 'kv'), may hold values from -0.5 to 0.5
- output_weight: bfloat16 [2048, 8192], P('kv', 'seq'), may hold values from -0.125 to 0.125
- key_cache_rows: bfloat16 [4, 2, 32768, 128], P('dp', 'kv', 'seq'), may hold values from -6000 to 6000, as said below
- value_cache_rows: bfloat16 [4, 2, 32768, 128], P('dp', 'kv', 'seq'), may hold values from -24 to 24
- live_lengths: int32 [4, 16], P('dp'), may hold values from 2 to 2048, as said below
- owner_shard: int32 [4], P('dp'), may hold values from 0 to 15
Outputs:
- layer_out: bfloat16 [4, 8192], P('dp', 'seq')
Inputs may be any that keep to these rules, and one draw needn't show every extreme that they name: `live_lengths`: every block holds 2 to 2048 live slots; the owner's block of a sequence holds fewer than 2048; in every sequence some other block holds exactly 2048. `key_cache_rows`: bounded as stated.
All inputs are finite; a program needn't handle non-finite values.
Results may differ from a plain program's by a relative error of at most 0.015.
The roundings to bfloat16 on the way count: a program that leaves them out, or rounds other values in their place, can miss the bound.
Values may be sent and summed in bfloat16 or wider, within the bound.
A program may use at most 64 MiB of HBM per device.

v0:
```python
import functools
import math

import jax
import jax.numpy as jnp
import numpy as np
from jax import lax
from jax.experimental import pallas as pl
from jax.experimental.pallas import tpu as pltpu
from jax.sharding import PartitionSpec as P

ROPE_THETA = 500000.0
F32 = jnp.float32
BF16 = jnp.bfloat16


def gather_start(buf, rank, count, send_sem, recv_sem, peer_of):
    copies = []
    for d in range(1, count):
        j = lax.rem(rank + d, count)
        cp = pltpu.make_async_remote_copy(
            src_ref=buf.at[rank],
            dst_ref=buf.at[rank],
            send_sem=send_sem.at[d],
            recv_sem=recv_sem.at[rank],
            device_id=peer_of(j),
            device_id_type=pl.DeviceIdType.MESH,
        )
        cp.start()
        copies.append(cp)
    return copies


def gather_wait(buf, rank, count, send_sem, recv_sem, peer_of):
    for d in range(1, count):
        j = lax.rem(rank + d, count)
        pltpu.make_async_remote_copy(
            src_ref=buf.at[j],
            dst_ref=buf.at[j],
            send_sem=send_sem.at[d],
            recv_sem=recv_sem.at[j],
            device_id=peer_of(j),
            device_id_type=pl.DeviceIdType.MESH,
        ).wait_recv()


def kernel(
    n, inner, outer, kv_size, group, head,
    live, owner, freq, x_hbm, wq_hbm, wkv_hbm, wo_hbm, k_hbm, v_hbm,
    out,
    x, wq, wkv, wo, keys, vals,
    part_in, part_out, acc_all, stat_all, kv_buf, q_rows, att_rows,
    load_sem, sa, ra, sb, rb, sc, rc, sd, rd, se, re, relay_sem,
):
    me = lax.axis_index("seq")
    kv = lax.axis_index("kv")
    batch = x.shape[0]
    rows = wq.shape[0]
    qw = wq.shape[1]
    slots = keys.shape[2]
    plane = me // inner
    spot = lax.rem(me, inner)

    def inner_peer(j):
        return {"seq": plane * inner + j}

    def outer_peer(j):
        return {"seq": j * inner + spot}

    def seq_peer(j):
        return {"seq": j}

    def kv_peer(j):
        return {"kv": j}

    barrier = pltpu.get_barrier_semaphore()
    for d in range(1, inner):
        pl.semaphore_signal(barrier, inc=1, device_id=inner_peer(lax.rem(spot + d, inner)),
                            device_id_type=pl.DeviceIdType.MESH)
    steps = [1 << i for i in range(outer.bit_length() - 1)]

    def across(step):
        return outer_peer(plane + step - 2 * step * lax.rem(plane // step, 2))

    for step in steps:
        pl.semaphore_signal(barrier, inc=1, device_id=across(step),
                            device_id_type=pl.DeviceIdType.MESH)
    for d in range(1, kv_size):
        pl.semaphore_signal(barrier, inc=1, device_id=kv_peer(lax.rem(kv + d, kv_size)),
                            device_id_type=pl.DeviceIdType.MESH)

    first = pl.multiple_of(me * rows, rows)
    loads = [
        pltpu.make_async_copy(x_hbm.at[:, pl.ds(first, rows)], x, load_sem.at[0]),
        pltpu.make_async_copy(wq_hbm, wq, load_sem.at[1]),
        pltpu.make_async_copy(wkv_hbm, wkv, load_sem.at[2]),
        pltpu.make_async_copy(k_hbm, keys, load_sem.at[3]),
        pltpu.make_async_copy(v_hbm, vals, load_sem.at[4]),
        pltpu.make_async_copy(wo_hbm, wo, load_sem.at[5]),
    ]
    for cp in loads[:3]:
        cp.start()

    row_id = lax.broadcasted_iota(jnp.int32, (batch, head), 0)
    lane_id = lax.broadcasted_iota(jnp.int32, (batch, head), 1)
    position = jnp.zeros((batch, head), jnp.int32)
    for b in range(batch):
        own = owner[b]
        position = jnp.where(row_id == b, own * slots + live[b, own], position)
    angle = position.astype(F32) * freq[...]
    cosine = jnp.cos(angle)
    sine = jnp.sin(angle)
    sine = jnp.where(lane_id < head // 2, -sine, sine)

    def rotate(v):
        return v * cosine + pltpu.roll(v, head // 2, 1) * sine

    for cp in loads[:3]:
        cp.wait()
    for cp in loads[3:]:
        cp.start()
    xs = x[...]
    part_in[spot, :, :qw] = jnp.dot(xs, wq[...], preferred_element_type=F32)
    part_in[spot, :, qw:] = jnp.dot(xs, wkv[...], preferred_element_type=F32)
    pl.semaphore_wait(barrier, inner - 1 + len(steps) + kv_size - 1)

    sends = gather_start(part_in, spot, inner, sa, ra, inner_peer)
    for i in range(len(steps) - 1):
        for step in steps:
            pl.semaphore_signal(relay_sem.at[i], inc=1, device_id=across(step),
                                device_id_type=pl.DeviceIdType.MESH)
        pl.semaphore_wait(relay_sem.at[i], len(steps))
    gather_wait(part_in, spot, inner, sa, ra, inner_peer)
    total = part_in[0]
    for j in range(1, inner):
        total = total + part_in[j]
    part_out[plane] = total
    sends += gather_start(part_out, plane, outer, sb, rb, outer_peer)
    gather_wait(part_out, plane, outer, sb, rb, outer_peer)
    total = part_out[0]
    for j in range(1, outer):
        total = total + part_out[j]

    for h in range(group):
        q_rows[:, h, :] = rotate(total[:, h * head:(h + 1) * head])
    key_new = rotate(total[:, qw:qw + head]).astype(BF16).astype(F32)
    value_new = total[:, qw + head:qw + 2 * head].astype(BF16).astype(F32)

    loads[3].wait()
    loads[4].wait()
    scaling = 1.0 / math.sqrt(head)
    slot_id = lax.broadcasted_iota(jnp.int32, (group, slots), 1)
    stat_lane = lax.broadcasted_iota(jnp.int32, (group, head), 1)
    stat_row = lax.broadcasted_iota(jnp.int32, (group, head), 0)
    pairs = batch * group
    stat = jnp.zeros((group, head), F32)
    accs = []
    for b in range(batch):
        q = q_rows[b].astype(BF16)
        new_score = jnp.sum(q.astype(F32) * key_new[b:b + 1], -1, keepdims=True) * scaling
        new_score = jnp.where(owner[b] == me, new_score, -jnp.inf)
        s = lax.dot_general(q, keys[b, 0], (((1,), (1,)), ((), ())), preferred_element_type=F32)
        s = jnp.where(slot_id < live[b, me], s * scaling, -jnp.inf)
        top = jnp.maximum(jnp.max(s, -1, keepdims=True), new_score)
        prob = jnp.exp(s - top).astype(BF16)
        new_prob = jnp.exp(new_score - top).astype(BF16).astype(F32)
        count = jnp.sum(prob.astype(F32), -1, keepdims=True) + new_prob
        acc = jnp.dot(prob, vals[b, 0], preferred_element_type=F32)
        accs.append(acc + new_prob * value_new[b:b + 1])
        stat = jnp.where(stat_lane == b * group + stat_row, top, stat)
        stat = jnp.where(stat_lane == pairs + b * group + stat_row, count, stat)
    stat_all[me] = jnp.sum(stat, 0, keepdims=True)
    acc_all[me] = jnp.concatenate(accs, 0).astype(BF16)

    sends += gather_start(stat_all, me, n, sd, rd, seq_peer)
    sends += gather_start(acc_all, me, n, sc, rc, seq_peer)
    gather_wait(stat_all, me, n, sd, rd, seq_peer)
    stats = stat_all[:, 0, :]
    factor = jnp.exp(stats - jnp.max(stats, 0, keepdims=True))
    whole = jnp.sum(factor * pltpu.roll(stats, head - pairs, 1), 0, keepdims=True)
    lane = lax.broadcasted_iota(jnp.int32, stats.shape, 1)
    weight = jnp.where(lane < pairs, factor / whole, 0.0).T
    gather_wait(acc_all, me, n, sc, rc, seq_peer)
    total = weight[:pairs, 0:1] * acc_all[0].astype(F32)
    for j in range(1, n):
        total = total + weight[:pairs, j:j + 1] * acc_all[j].astype(F32)
    for b in range(batch):
        att_rows[b] = total[b * group:(b + 1) * group]
    attended = jnp.concatenate([att_rows[:, h, :].astype(BF16) for h in range(group)], -1)

    loads[5].wait()
    kv_buf[kv] = jnp.dot(attended, wo[...], preferred_element_type=F32)
    sends += gather_start(kv_buf, kv, kv_size, se, re, kv_peer)
    gather_wait(kv_buf, kv, kv_size, se, re, kv_peer)
    total = kv_buf[0]
    for j in range(1, kv_size):
        total = total + kv_buf[j]
    out[...] = total
    for cp in sends:
        cp.wait_send()


def local(n, kv_size, x, wq, wkv, wo, keys, vals, live, owner):
    batch = x.shape[0]
    head = keys.shape[3]
    rows, qw = wq.shape
    group = qw // head
    cols = wo.shape[1]
    inner = 1
    while inner * inner < n and n % (inner * 2) == 0:
        inner *= 2
    outer = n // inner
    half = np.float64(ROPE_THETA) ** (-np.arange(0, head, 2, dtype=np.float64) / head)
    freq = jnp.asarray(np.concatenate([half, half]).astype(np.float32)[None, :])
    dma = pltpu.SemaphoreType.DMA
    smem = pl.BlockSpec(memory_space=pltpu.SMEM)
    vmem = pl.BlockSpec(memory_space=pltpu.VMEM)
    hbm = pl.BlockSpec(memory_space=pl.ANY)
    return pl.pallas_call(
        functools.partial(kernel, n, inner, outer, kv_size, group, head),
        out_shape=pltpu.VMEM((batch, cols), F32),
        in_specs=[smem, smem, vmem] + [hbm] * 6,
        out_specs=vmem,
        scratch_shapes=[
            pltpu.VMEM((batch, rows), BF16),
            pltpu.VMEM(wq.shape, BF16),
            pltpu.VMEM(wkv.shape, BF16),
            pltpu.VMEM(wo.shape, BF16),
            pltpu.VMEM(keys.shape, BF16),
            pltpu.VMEM(vals.shape, BF16),
            pltpu.VMEM((inner, batch, qw + wkv.shape[1]), F32),
            pltpu.VMEM((outer, batch, qw + wkv.shape[1]), F32),
            pltpu.VMEM((n, batch * group, head), BF16),
            pltpu.VMEM((n, 1, head), F32),
            pltpu.VMEM((kv_size, batch, cols), F32),
            pltpu.VMEM((batch, group, head), F32),
            pltpu.VMEM((batch, group, head), F32),
            dma((6,)),
            dma((inner,)), dma((inner,)),
            dma((outer,)), dma((outer,)),
            dma((n,)), dma((n,)),
            dma((n,)), dma((n,)),
            dma((kv_size,)), dma((kv_size,)),
            pltpu.SemaphoreType.REGULAR((max(outer.bit_length() - 2, 1),)),
        ],
        compiler_params=pltpu.CompilerParams(collective_id=0, has_side_effects=True),
    )(live, owner, freq, x, wq, wkv, wo, keys, vals).astype(BF16)


def solution(mesh):
    return jax.shard_map(
        functools.partial(local, mesh.shape["seq"], mesh.shape["kv"]),
        mesh=mesh,
        in_specs=(
            P("dp", None),
            P("seq", "kv"),
            P("seq", "kv"),
            P("kv", "seq"),
            P("dp", "kv", "seq", None),
            P("dp", "kv", "seq", None),
            P("dp", None),
            P("dp"),
        ),
        out_specs=P("dp", "seq"),
        check_vma=False,
    )
```

profile of v0, /device:TPU:0, one launch (start us, length us, event | category | flops | bytes accessed | tf_op | source)
XLA Modules:
  0.0 21.9 jit_solution(16805728927854783607)
XLA Ops:
  0.0 21.3 %shard_map.91 = f32[4,512]{1,0:T(4,128)S(1)} custom-call(s32[4,16]{1,0:T(4,128)} %live.1, s32[4]{0:T(128)} %owner.1, f32[1,128]{1,0:T(1,128)} %constant.2.clone.freq, bf16[4,8192]{1,0:T(4,128)(2,1)} %x_hbm.1, bf16[512,1024]{1,0:T(8,128)(2,1)} %wq_hbm.1, bf16[512,256]{1,0:T(8,128)(2,1)} %wkv_hbm.1, bf16[1024,512]{1,0:T(8,128)(2,1)} %wo_hbm.1, ...), custom_call_target="tpu_custom_call" | custom-call | tf_op jit(solution)/shard_map/pallas_call | solution.py:219
  21.3 0.6 %convert_element_type.3 = bf16[4,512]{1,0:T(4,128)(2,1)} convert(f32[4,512]{1,0:T(4,128)S(1)} %shard_map.91) | non-fusion elementwise | flops 2048 | bytes 12288 | tf_op jit(solution)/shard_map/convert_element_type | solution.py:247
where the time goes:
time: 22.1 us; the launch traced here: 21.9 us
  Pallas kernels  21.3 us (96%)
  other arithmetic  0.6 us (3%)
    pallas_call x1, Pallas kernels, local(): pl.pallas_call(functools.partial(kernel, n, inner, outer, kv_size, group,...  21.3 us
    convert_element_type x1, other arithmetic, local(): return pl.pallas_call(functools.partial(kernel, n, inner, outer, kv_size,...  0.6 us

commit v1 on v0

v1 whole, which is shorter than its diff:
```python
import functools
import math

import jax
import jax.numpy as jnp
import numpy as np
from jax import lax
from jax.experimental import pallas as pl
from jax.experimental.pallas import tpu as pltpu
from jax.sharding import PartitionSpec as P

ROPE_THETA = 500000.0
F32 = jnp.float32
BF16 = jnp.bfloat16
MESH = pl.DeviceIdType.MESH
CHUNKS = 2


def kernel(
    n, inner, outer, group, head,
    live_hbm, owner_hbm, freq_hbm, x_hbm, wq_hbm, wkv_hbm, wo_hbm, k_hbm, v_hbm,
    out,
    live, owner, freq, x, wq, wkv, wo, keys, keys_t, vals,
    part, a_in, a_sum, b_in, acc_out, acc_in, stat_out, stat_in, kv_buf, att_rows,
    load_sem, a_recv, b_recv, g_recv, send_sem, stat_recv, wo_recv, kv_recv, ready,
):
    me = lax.axis_index("seq")
    kv = lax.axis_index("kv")
    other = 1 - kv
    batch = x.shape[0]
    rows = wq.shape[0]
    qw = wq.shape[1]
    slots = keys.shape[2]
    per = batch // CHUNKS
    pairs = batch * group
    plane = me // inner
    spot = lax.rem(me, inner)
    partner = {"kv": other}
    steps = [1 << i for i in range(outer.bit_length() - 1)]

    def flipped(j):
        return {"seq": j, "kv": other}

    def across(step):
        return {"seq": (plane + step - 2 * step * lax.rem(plane // step, 2)) * inner + spot}

    def signal(sem, device):
        pl.semaphore_signal(sem, inc=1, device_id=device, device_id_type=MESH)

    def push(src, dst, send, recv, device):
        pltpu.make_async_remote_copy(
            src_ref=src, dst_ref=dst, send_sem=send, recv_sem=recv,
            device_id=device, device_id_type=MESH,
        ).start()

    def arrived(buf, recv):
        pltpu.make_async_remote_copy(
            src_ref=buf, dst_ref=buf, send_sem=send_sem.at[0], recv_sem=recv,
            device_id=partner, device_id_type=MESH,
        ).wait_recv()

    def sent(buf, send):
        pltpu.make_async_remote_copy(
            src_ref=buf, dst_ref=buf, send_sem=send, recv_sem=a_recv.at[0],
            device_id=partner, device_id_type=MESH,
        ).wait_send()

    first = pl.multiple_of(me * rows, rows)
    half = rows // 2
    loads = [
        pltpu.make_async_copy(x_hbm.at[:, pl.ds(first, rows)], x, load_sem.at[0]),
        pltpu.make_async_copy(wq_hbm.at[pl.ds(0, half)], wq.at[pl.ds(0, half)], load_sem.at[1]),
        pltpu.make_async_copy(wq_hbm.at[pl.ds(half, half)], wq.at[pl.ds(half, half)], load_sem.at[2]),
        pltpu.make_async_copy(wkv_hbm, wkv, load_sem.at[3]),
        pltpu.make_async_copy(live_hbm, live, load_sem.at[4]),
        pltpu.make_async_copy(owner_hbm, owner, load_sem.at[5]),
        pltpu.make_async_copy(freq_hbm, freq, load_sem.at[6]),
        pltpu.make_async_copy(k_hbm, keys, load_sem.at[7]),
        pltpu.make_async_copy(v_hbm, vals, load_sem.at[8]),
    ]
    for cp in loads[:7]:
        cp.start()

    barrier = pltpu.get_barrier_semaphore()
    signal(barrier, partner)
    for d in range(1, inner):
        signal(barrier, flipped(plane * inner + lax.rem(spot + d, inner)))
    for step in steps:
        signal(barrier, across(step))

    loads[0].wait()
    loads[1].wait()
    low = jnp.dot(x[:, :half], wq[:half, :], preferred_element_type=F32)
    loads[2].wait()
    loads[3].wait()
    loads[7].start()
    loads[8].start()
    projected = low + jnp.dot(x[:, half:], wq[half:, :], preferred_element_type=F32)
    both = jnp.dot(x[...], wkv[...], preferred_element_type=F32)
    for h in range(group):
        part[:, h, :] = projected[:, h * head:(h + 1) * head]
    part[:, group, :] = both[:, :head]
    part[:, group + 1, :] = both[:, head:]
    pl.semaphore_wait(barrier, inner + len(steps))

    for c in range(CHUNKS):
        for d in list(range(1, inner)) + [0]:
            j = plane * inner + lax.rem(spot + d, inner)
            push(part.at[pl.ds(c * per, per)], a_in.at[c, spot], send_sem.at[0], a_recv.at[c], flipped(j))

    for cp in loads[4:7]:
        cp.wait()
    row_id = lax.broadcasted_iota(jnp.int32, (batch, head), 0)
    lane_id = lax.broadcasted_iota(jnp.int32, (batch, head), 1)
    position = jnp.zeros((batch, head), jnp.int32)
    for b in range(batch):
        own = owner[b]
        position = jnp.where(row_id == b, own * slots + live[b, own], position)
    angle = position.astype(F32) * freq[...]
    cosine = jnp.cos(angle)
    sine = jnp.sin(angle)
    sine = jnp.where(lane_id < head // 2, -sine, sine)

    def rotate(v, b):
        return v * cosine[b:b + 1] + pltpu.roll(v, head // 2, 1) * sine[b:b + 1]

    for i in range(max(len(steps) - 1, 1)):
        for step in steps:
            signal(ready.at[2 + i], across(step))
        if i == 0:
            loads[7].wait()
            for b in range(batch):
                keys_t[b] = keys[b, 0].T
        pl.semaphore_wait(ready.at[2 + i], len(steps))
    signal(ready.at[0], partner)
    pl.semaphore_wait(ready.at[0], 1)

    for c in range(CHUNKS):
        arrived(a_in.at[c], a_recv.at[c])
        total = a_in[c, 0]
        for j in range(1, inner):
            total = total + a_in[c, j]
        a_sum[c * per:(c + 1) * per] = total
        for d in list(range(1, outer)) + [0]:
            j = lax.rem(plane + d, outer) * inner + spot
            push(a_sum.at[pl.ds(c * per, per)], b_in.at[c, plane], send_sem.at[1], b_recv.at[c], flipped(j))
    push(wo_hbm, wo, send_sem.at[2], wo_recv.at[0], partner)
    loads[8].wait()

    scaling = 1.0 / math.sqrt(head)
    slot_id = lax.broadcasted_iota(jnp.int32, (group, slots), 1)
    stat_lane = lax.broadcasted_iota(jnp.int32, (group, head), 1)
    stat_row = lax.broadcasted_iota(jnp.int32, (group, head), 0)
    stat = jnp.zeros((group, head), F32)
    raw = []
    for c in range(CHUNKS):
        arrived(b_in.at[c], b_recv.at[c])
        total = b_in[c, 0]
        for j in range(1, outer):
            total = total + b_in[c, j]
        for i in range(per):
            b = c * per + i
            q = rotate(total[i, :group], b).astype(BF16)
            key_new = rotate(total[i, group:group + 1], b).astype(BF16).astype(F32)
            value_new = total[i, group + 1:group + 2].astype(BF16).astype(F32)
            s = jnp.dot(q, keys_t[b], preferred_element_type=F32)
            raw.append((q, key_new, value_new, s))
    signal(ready.at[1], partner)
    order = sorted(range(n), key=lambda d: (abs(d - n // 2), d))
    for c in range(CHUNKS):
        accs = []
        for i in range(per):
            b = c * per + i
            q, key_new, value_new, s = raw[b]
            new_score = jnp.sum(q.astype(F32) * key_new, -1, keepdims=True) * scaling
            new_score = jnp.where(owner[b] == me, new_score, -jnp.inf)
            s = jnp.where(slot_id < live[b, me], s * scaling, -jnp.inf)
            top = jnp.maximum(jnp.max(s, -1, keepdims=True), new_score)
            prob = jnp.exp(s - top).astype(BF16)
            new_prob = jnp.exp(new_score - top).astype(BF16).astype(F32)
            count = jnp.sum(prob.astype(F32), -1, keepdims=True) + new_prob
            acc = jnp.dot(prob, vals[b, 0], preferred_element_type=F32)
            accs.append(acc + new_prob * value_new)
            stat = jnp.where(stat_lane == b * group + stat_row, top, stat)
            stat = jnp.where(stat_lane == pairs + b * group + stat_row, count, stat)
        acc_out[c] = jnp.concatenate(accs, 0).astype(BF16)
        if c == 0:
            pl.semaphore_wait(ready.at[1], 1)
        if c == CHUNKS - 1:
            stat_out[...] = jnp.sum(stat, 0, keepdims=True)
            for d in order:
                push(stat_out, stat_in.at[me], send_sem.at[4], stat_recv.at[0], flipped(lax.rem(me + d, n)))
        for d in order:
            push(acc_out.at[c], acc_in.at[c, me], send_sem.at[3], g_recv.at[c], flipped(lax.rem(me + d, n)))

    arrived(stat_in, stat_recv.at[0])
    stats = stat_in[:, 0, :]
    factor = jnp.exp(stats - jnp.max(stats, 0, keepdims=True))
    whole = jnp.sum(factor * pltpu.roll(stats, head - pairs, 1), 0, keepdims=True)
    lane = lax.broadcasted_iota(jnp.int32, stats.shape, 1)
    weight = jnp.where(lane < pairs, factor / whole, 0.0).T
    for c in range(CHUNKS):
        arrived(acc_in.at[c], g_recv.at[c])
        low_row = c * per * group
        high_row = low_row + per * group
        total = weight[low_row:high_row, 0:1] * acc_in[c, 0].astype(F32)
        for j in range(1, n):
            total = total + weight[low_row:high_row, j:j + 1] * acc_in[c, j].astype(F32)
        for i in range(per):
            att_rows[c * per + i] = total[i * group:(i + 1) * group]
    attended = jnp.concatenate([att_rows[:, h, :].astype(BF16) for h in range(group)], -1)

    arrived(wo, wo_recv.at[0])
    kv_buf[other] = jnp.dot(attended, wo[...], preferred_element_type=F32)
    push(kv_buf.at[other], kv_buf.at[other], send_sem.at[5], kv_recv.at[0], partner)
    arrived(kv_buf.at[kv], kv_recv.at[0])
    out[...] = kv_buf[0] + kv_buf[1]
    sent(a_in, send_sem.at[0])
    sent(b_in, send_sem.at[1])
    sent(wo, send_sem.at[2])
    sent(acc_in, send_sem.at[3])
    sent(stat_in, send_sem.at[4])
    sent(kv_buf.at[0], send_sem.at[5])


def local(n, x, wq, wkv, wo, keys, vals, live, owner):
    batch = x.shape[0]
    head = keys.shape[3]
    slots = keys.shape[2]
    rows, qw = wq.shape
    group = qw // head
    cols = wo.shape[1]
    inner = 1
    while inner * inner < n and n % (inner * 2) == 0:
        inner *= 2
    outer = n // inner
    per = batch // CHUNKS
    half = np.float64(ROPE_THETA) ** (-np.arange(0, head, 2, dtype=np.float64) / head)
    freq = jnp.asarray(np.concatenate([half, half]).astype(np.float32)[None, :])
    dma = pltpu.SemaphoreType.DMA
    vmem = pl.BlockSpec(memory_space=pltpu.VMEM)
    hbm = pl.BlockSpec(memory_space=pl.ANY)
    rounds = max(outer.bit_length() - 2, 1)
    return pl.pallas_call(
        functools.partial(kernel, n, inner, outer, group, head),
        out_shape=pltpu.VMEM((batch, cols), F32),
        in_specs=[hbm] * 9,
        out_specs=vmem,
        scratch_shapes=[
            pltpu.SMEM(live.shape, jnp.int32),
            pltpu.SMEM(owner.shape, jnp.int32),
            pltpu.VMEM((1, head), F32),
            pltpu.VMEM((batch, rows), BF16),
            pltpu.VMEM(wq.shape, BF16),
            pltpu.VMEM(wkv.shape, BF16),
            pltpu.VMEM(wo.shape, BF16),
            pltpu.VMEM(keys.shape, BF16),
            pltpu.VMEM((batch, head, slots), BF16),
            pltpu.VMEM(vals.shape, BF16),
            pltpu.VMEM((batch, group + 2, head), F32),
            pltpu.VMEM((CHUNKS, inner, per, group + 2, head), F32),
            pltpu.VMEM((batch, group + 2, head), F32),
            pltpu.VMEM((CHUNKS, outer, per, group + 2, head), F32),
            pltpu.VMEM((CHUNKS, per * group, head), BF16),
            pltpu.VMEM((CHUNKS, n, per * group, head), BF16),
            pltpu.VMEM((1, head), F32),
            pltpu.VMEM((n, 1, head), F32),
            pltpu.VMEM((2, batch, cols), F32),
            pltpu.VMEM((batch, group, head), F32),
            dma((9,)),
            dma((CHUNKS,)), dma((CHUNKS,)), dma((CHUNKS,)),
            dma((6,)),
            dma((1,)), dma((1,)), dma((1,)),
            pltpu.SemaphoreType.REGULAR((2 + rounds,)),
        ],
        compiler_params=pltpu.CompilerParams(collective_id=0, has_side_effects=True),
    )(live, owner, freq, x, wq, wkv, wo, keys, vals).astype(BF16)


def solution(mesh):
    return jax.shard_map(
        functools.partial(local, mesh.shape["seq"]),
        mesh=mesh,
        in_specs=(
            P("dp", None),
            P("seq", "kv"),
            P("seq", "kv"),
            P("kv", "seq"),
            P("dp", "kv", "seq", None),
            P("dp", "kv", "seq", None),
            P("dp", None),
            P("dp"),
        ),
        out_specs=P("dp", "seq"),
        check_vma=False,
    )
```

time: 22.1 us -> 20.5 us (0.928)
  Pallas kernels: 21.3 us -> 19.7 us
    pallas_call x1, Pallas kernels: 21.3 us -> 19.7 us  [local(): pl.pallas_call(functools.partial(kernel, n, inner, outer, group, head), o...]
where the time goes in v1:
time: 20.5 us; the launch traced here: 20.3 us
  Pallas kernels  19.7 us (96%)
  other arithmetic  0.6 us (3%)
    pallas_call x1, Pallas kernels, local(): pl.pallas_call(functools.partial(kernel, n, inner, outer, group, head), o...  19.7 us
    convert_element_type x1, other arithmetic, local(): return pl.pallas_call(functools.partial(kernel, n, inner, outer, group, h...  0.6 us

profile of v1, /device:TPU:0, one launch (start us, length us, event | category | flops | bytes accessed | tf_op | source)
XLA Modules:
  0.0 20.3 jit_solution(596860365511721298)
XLA Ops:
  0.0 19.7 %shard_map.91 = f32[4,512]{1,0:T(4,128)S(1)} custom-call(s32[4,16]{1,0:T(4,128)} %live_hbm.1, s32[4]{0:T(128)} %owner_hbm.1, f32[1,128]{1,0:T(1,128)} %constant.2.clone.freq_hbm, bf16[4,8192]{1,0:T(4,128)(2,1)} %x_hbm.1, bf16[512,1024]{1,0:T(8,128)(2,1)} %wq_hbm.1, bf16[512,256]{1,0:T(8,128)(2,1)} %wkv_hbm.1, bf16[1024,512]{1,0:T(8,128)(2,1)} %wo_hbm.1, ...), custom_call_target="tpu_custom_call" | custom-call | tf_op jit(solution)/shard_map/pallas_call | solution.py:244
  19.7 0.6 %convert_element_type.3 = bf16[4,512]{1,0:T(4,128)(2,1)} convert(f32[4,512]{1,0:T(4,128)S(1)} %shard_map.91) | non-fusion elementwise | flops 2048 | bytes 12288 | tf_op jit(solution)/shard_map/convert_element_type | solution.py:277

commit v2 on v1

v2 whole, which is shorter than its diff:
```python
import functools
import math

import jax
import jax.numpy as jnp
import numpy as np
from jax import lax
from jax.experimental import pallas as pl
from jax.experimental.pallas import tpu as pltpu
from jax.sharding import PartitionSpec as P

ROPE_THETA = 500000.0
F32 = jnp.float32
BF16 = jnp.bfloat16
MESH = pl.DeviceIdType.MESH
CHUNKS = 2
PARTS = 2
PIECES = 4


def kernel(
    n, inner, outer, group, head,
    live_hbm, owner_hbm, freq_hbm, x_hbm, wq_hbm, wkv_hbm, wo_hbm, k_hbm, v_hbm,
    out,
    live, owner, freq, x, wq, wkv, wo, keys, keys_t, vals,
    part, part_new, a_in, a_new, a_sum, sum_new, b_in, b_new,
    acc_out, acc_in, stat_out, stat_in, new_out, new_in, kv_buf, att_rows,
    load_sem, a_recv, b_recv, g_recv, send_sem, pair_recv, ready,
):
    me = lax.axis_index("seq")
    kv = lax.axis_index("kv")
    other = 1 - kv
    batch = x.shape[0]
    rows = wq.shape[0]
    qw = wq.shape[1]
    slots = keys.shape[2]
    per = batch // CHUNKS
    pairs = batch * group
    plane = me // inner
    spot = lax.rem(me, inner)
    partner = {"kv": other}
    steps = [1 << i for i in range(outer.bit_length() - 1)]

    def flipped(j):
        return {"seq": j, "kv": other}

    def across(step):
        return {"seq": (plane + step - 2 * step * lax.rem(plane // step, 2)) * inner + spot}

    def signal(sem, device):
        pl.semaphore_signal(sem, inc=1, device_id=device, device_id_type=MESH)

    def push(src, dst, send, recv, device):
        pltpu.make_async_remote_copy(
            src_ref=src, dst_ref=dst, send_sem=send, recv_sem=recv,
            device_id=device, device_id_type=MESH,
        ).start()

    def arrived(buf, recv):
        pltpu.make_async_remote_copy(
            src_ref=buf, dst_ref=buf, send_sem=send_sem.at[0], recv_sem=recv,
            device_id=partner, device_id_type=MESH,
        ).wait_recv()

    def sent(buf, send):
        pltpu.make_async_remote_copy(
            src_ref=buf, dst_ref=buf, send_sem=send, recv_sem=a_recv.at[0],
            device_id=partner, device_id_type=MESH,
        ).wait_send()

    def in_plane(src, dst, send, recv):
        for d in range(inner - 1, -1, -1):
            push(src, dst, send, recv, flipped(plane * inner + lax.bitwise_xor(spot, d)))

    def over_planes(src, dst, send, recv):
        for d in [outer // 2] + [d for d in range(1, outer) if d != outer // 2] + [0]:
            push(src, dst, send, recv, flipped(lax.rem(plane + d, outer) * inner + spot))

    first = pl.multiple_of(me * rows, rows)
    piece = rows // PIECES
    x_load = pltpu.make_async_copy(x_hbm.at[:, pl.ds(first, rows)], x, load_sem.at[0])
    q_loads = [
        pltpu.make_async_copy(wq_hbm.at[pl.ds(i * piece, piece)], wq.at[pl.ds(i * piece, piece)], load_sem.at[1 + i])
        for i in range(PIECES)
    ]
    later = [(wkv_hbm, wkv), (live_hbm, live), (owner_hbm, owner), (freq_hbm, freq), (k_hbm, keys), (v_hbm, vals)]
    kv_load, live_load, owner_load, freq_load, k_load, v_load = [
        pltpu.make_async_copy(src, dst, load_sem.at[1 + PIECES + i]) for i, (src, dst) in enumerate(later)
    ]
    x_load.start()
    for cp in q_loads:
        cp.start()
    kv_load.start()
    live_load.start()
    owner_load.start()
    freq_load.start()

    barrier = pltpu.get_barrier_semaphore()
    signal(barrier, partner)
    for d in range(1, inner):
        signal(barrier, flipped(plane * inner + lax.rem(spot + d, inner)))
    for step in steps:
        signal(barrier, across(step))

    x_load.wait()
    projected = None
    for i, cp in enumerate(q_loads):
        cp.wait()
        if i == PIECES - 1:
            k_load.start()
            v_load.start()
        term = jnp.dot(x[:, i * piece:(i + 1) * piece], wq[i * piece:(i + 1) * piece, :], preferred_element_type=F32)
        projected = term if projected is None else projected + term
    for h in range(group):
        part[:, h, :] = projected[:, h * head:(h + 1) * head]
    pl.semaphore_wait(barrier, inner + len(steps))

    for c in range(CHUNKS):
        in_plane(part.at[pl.ds(c * per, per)], a_in.at[c, spot], send_sem.at[0], a_recv.at[c])

    kv_load.wait()
    both = jnp.dot(x[...], wkv[...], preferred_element_type=F32)
    part_new[0] = both[:, :head]
    part_new[1] = both[:, head:]
    in_plane(part_new, a_new.at[spot], send_sem.at[0], a_recv.at[CHUNKS])

    live_load.wait()
    owner_load.wait()
    freq_load.wait()
    row_id = lax.broadcasted_iota(jnp.int32, (batch, head), 0)
    lane_id = lax.broadcasted_iota(jnp.int32, (batch, head), 1)
    position = jnp.zeros((batch, head), jnp.int32)
    for b in range(batch):
        own = owner[b]
        position = jnp.where(row_id == b, own * slots + live[b, own], position)
    angle = position.astype(F32) * freq[...]
    cosine = jnp.cos(angle)
    sine = jnp.sin(angle)
    sine = jnp.where(lane_id < head // 2, -sine, sine)

    for i in range(max(len(steps) - 1, 1)):
        for step in steps:
            signal(ready.at[2 + i], across(step))
        if i == 0:
            k_load.wait()
            for b in range(batch):
                keys_t[b] = keys[b, 0].T
        pl.semaphore_wait(ready.at[2 + i], len(steps))
    signal(ready.at[0], partner)
    pl.semaphore_wait(ready.at[0], 1)

    for c in range(CHUNKS):
        arrived(a_in.at[c], a_recv.at[c])
        total = a_in[c, 0]
        for j in range(1, inner):
            total = total + a_in[c, j]
        a_sum[c * per:(c + 1) * per] = total
        over_planes(a_sum.at[pl.ds(c * per, per)], b_in.at[c, plane], send_sem.at[0], b_recv.at[c])
    arrived(a_new, a_recv.at[CHUNKS])
    total = a_new[0]
    for j in range(1, inner):
        total = total + a_new[j]
    sum_new[...] = total
    over_planes(sum_new, b_new.at[plane], send_sem.at[0], b_recv.at[CHUNKS])
    push(wo_hbm, wo, send_sem.at[0], pair_recv.at[0], partner)
    v_load.wait()

    scaling = 1.0 / math.sqrt(head)
    slot_id = lax.broadcasted_iota(jnp.int32, (group, slots), 1)
    stat_lane = lax.broadcasted_iota(jnp.int32, (group, head), 1)
    stat_row = lax.broadcasted_iota(jnp.int32, (group, head), 0)
    stat = jnp.zeros((group, head), F32)
    queries = []
    order = [
        lax.rem(plane + dz, outer) * inner + lax.bitwise_xor(spot, ds)
        for ds in sorted(range(inner), key=lambda v: (v % 2 == 0, -v))
        for dz in sorted(range(outer), key=lambda v: -min(v, outer - v))
    ]
    scores = []
    for c in range(CHUNKS):
        arrived(b_in.at[c], b_recv.at[c])
        if c == 0:
            signal(ready.at[1], partner)
        total = b_in[c, 0]
        for j in range(1, outer):
            total = total + b_in[c, j]
        for i in range(per):
            b = c * per + i
            q = total[i] * cosine[b:b + 1] + pltpu.roll(total[i], head // 2, 1) * sine[b:b + 1]
            q = q.astype(BF16)
            queries.append(q)
            scores.append(jnp.dot(q, keys_t[b], preferred_element_type=F32))
    few = batch // PARTS
    for c in range(PARTS):
        accs = []
        for b in range(c * few, c * few + few):
            s = jnp.where(slot_id < live[b, me], scores[b] * scaling, -jnp.inf)
            top = jnp.max(s, -1, keepdims=True)
            prob = jnp.exp(s - top).astype(BF16)
            count = jnp.sum(prob.astype(F32), -1, keepdims=True)
            accs.append(jnp.dot(prob, vals[b, 0], preferred_element_type=F32))
            stat = jnp.where(stat_lane == b * group + stat_row, top, stat)
            stat = jnp.where(stat_lane == pairs + b * group + stat_row, count, stat)
        acc_out[c] = jnp.concatenate(accs, 0).astype(BF16)
        if c == 0:
            pl.semaphore_wait(ready.at[1], 1)
        if c == PARTS - 1:
            stat_out[...] = jnp.sum(stat, 0, keepdims=True)
            for j in order:
                push(stat_out, stat_in.at[me], send_sem.at[0], pair_recv.at[3], flipped(j))
        for j in order:
            push(acc_out.at[c], acc_in.at[c, me], send_sem.at[0], g_recv.at[c], flipped(j))

    arrived(b_new, b_recv.at[CHUNKS])
    total = b_new[0]
    for j in range(1, outer):
        total = total + b_new[j]
    key_new = total[0] * cosine + pltpu.roll(total[0], head // 2, 1) * sine
    key_new = key_new.astype(BF16).astype(F32)
    fresh = jnp.where(stat_lane >= pairs, 1.0 / group, 0.0)
    for b in range(batch):
        score = jnp.sum(queries[b].astype(F32) * key_new[b:b + 1], -1, keepdims=True) * scaling
        fresh = jnp.where(stat_lane == b * group + stat_row, score, fresh)
    new_out[:batch] = total[1].astype(BF16).astype(F32)
    new_out[batch:batch + 1] = jnp.sum(fresh, 0, keepdims=True)
    push(new_out, new_in, send_sem.at[0], pair_recv.at[1], partner)

    arrived(stat_in, pair_recv.at[3])
    arrived(new_in, pair_recv.at[1])
    stats = stat_in[:, 0, :]
    newest = new_in[batch:batch + 1]
    top = jnp.maximum(jnp.max(stats, 0, keepdims=True), newest)
    factor = jnp.exp(stats - top)
    fresh = jnp.exp(newest - top)
    whole = jnp.sum(factor * pltpu.roll(stats, head - pairs, 1), 0, keepdims=True) + fresh
    lane = lax.broadcasted_iota(jnp.int32, stats.shape, 1)
    weight = jnp.where(lane < pairs, factor / whole, 0.0).T
    fresh = jnp.where(lane[:1] < pairs, fresh / whole, 0.0)
    fresh = jnp.broadcast_to(fresh, (group, head)).T
    for c in range(PARTS):
        arrived(acc_in.at[c], g_recv.at[c])
        low_row = c * few * group
        high_row = low_row + few * group
        total = weight[low_row:high_row, 0:1] * acc_in[c, 0].astype(F32)
        for j in range(1, n):
            total = total + weight[low_row:high_row, j:j + 1] * acc_in[c, j].astype(F32)
        for i in range(few):
            b = c * few + i
            own = fresh[b * group:(b + 1) * group, 0:1] * new_in[b:b + 1]
            att_rows[b] = total[i * group:(i + 1) * group] + own
    attended = jnp.concatenate([att_rows[:, h, :].astype(BF16) for h in range(group)], -1)

    arrived(wo, pair_recv.at[0])
    kv_buf[other] = jnp.dot(attended, wo[...], preferred_element_type=F32)
    push(kv_buf.at[other], kv_buf.at[other], send_sem.at[0], pair_recv.at[2], partner)
    arrived(kv_buf.at[kv], pair_recv.at[2])
    out[...] = kv_buf[0] + kv_buf[1]
    sent(a_in, send_sem.at[0])
    sent(b_in, send_sem.at[0])
    sent(a_new, send_sem.at[0])
    sent(b_new, send_sem.at[0])
    sent(wo, send_sem.at[0])
    sent(acc_in, send_sem.at[0])
    sent(stat_in, send_sem.at[0])
    sent(new_in, send_sem.at[0])
    sent(kv_buf.at[0], send_sem.at[0])


def local(n, x, wq, wkv, wo, keys, vals, live, owner):
    batch = x.shape[0]
    head = keys.shape[3]
    slots = keys.shape[2]
    rows, qw = wq.shape
    group = qw // head
    cols = wo.shape[1]
    inner = 1
    while inner * inner < n and n % (inner * 2) == 0:
        inner *= 2
    outer = n // inner
    per = batch // CHUNKS
    half = np.float64(ROPE_THETA) ** (-np.arange(0, head, 2, dtype=np.float64) / head)
    freq = jnp.asarray(np.concatenate([half, half]).astype(np.float32)[None, :])
    dma = pltpu.SemaphoreType.DMA
    vmem = pl.BlockSpec(memory_space=pltpu.VMEM)
    hbm = pl.BlockSpec(memory_space=pl.ANY)
    rounds = max(outer.bit_length() - 2, 1)
    return pl.pallas_call(
        functools.partial(kernel, n, inner, outer, group, head),
        out_shape=pltpu.VMEM((batch, cols), F32),
        in_specs=[hbm] * 9,
        out_specs=vmem,
        scratch_shapes=[
            pltpu.SMEM(live.shape, jnp.int32),
            pltpu.SMEM(owner.shape, jnp.int32),
            pltpu.VMEM((1, head), F32),
            pltpu.VMEM((batch, rows), BF16),
            pltpu.VMEM(wq.shape, BF16),
            pltpu.VMEM(wkv.shape, BF16),
            pltpu.VMEM(wo.shape, BF16),
            pltpu.VMEM(keys.shape, BF16),
            pltpu.VMEM((batch, head, slots), BF16),
            pltpu.VMEM(vals.shape, BF16),
            pltpu.VMEM((batch, group, head), F32),
            pltpu.VMEM((2, batch, head), F32),
            pltpu.VMEM((CHUNKS, inner, per, group, head), F32),
            pltpu.VMEM((inner, 2, batch, head), F32),
            pltpu.VMEM((batch, group, head), F32),
            pltpu.VMEM((2, batch, head), F32),
            pltpu.VMEM((CHUNKS, outer, per, group, head), F32),
            pltpu.VMEM((outer, 2, batch, head), F32),
            pltpu.VMEM((PARTS, batch // PARTS * group, head), BF16),
            pltpu.VMEM((PARTS, n, batch // PARTS * group, head), BF16),
            pltpu.VMEM((1, head), F32),
            pltpu.VMEM((n, 1, head), F32),
            pltpu.VMEM((batch + 1, head), F32),
            pltpu.VMEM((batch + 1, head), F32),
            pltpu.VMEM((2, batch, cols), F32),
            pltpu.VMEM((batch, group, head), F32),
            dma((7 + PIECES,)),
            dma((CHUNKS + 1,)), dma((CHUNKS + 1,)), dma((PARTS,)),
            dma((1,)),
            dma((4,)),
            pltpu.SemaphoreType.REGULAR((2 + rounds,)),
        ],
        compiler_params=pltpu.CompilerParams(collective_id=0, has_side_effects=True),
    )(live, owner, freq, x, wq, wkv, wo, keys, vals).astype(BF16)


def solution(mesh):
    return jax.shard_map(
        functools.partial(local, mesh.shape["seq"]),
        mesh=mesh,
        in_specs=(
            P("dp", None),
            P("seq", "kv"),
            P("seq", "kv"),
            P("kv", "seq"),
            P("dp", "kv", "seq", None),
            P("dp", "kv", "seq", None),
            P("dp", None),
            P("dp"),
        ),
        out_specs=P("dp", "seq"),
        check_vma=False,
    )
```

time: 20.5 us -> 19.6 us (0.956)
  Pallas kernels: 19.7 us -> 18.8 us
    pallas_call x1, Pallas kernels: 19.7 us -> 18.8 us  [local(): pl.pallas_call(functools.partial(kernel, n, inner, outer, group, head), o...]
where the time goes in v2:
time: 19.6 us; the launch traced here: 19.4 us
  Pallas kernels  18.8 us (96%)
  other arithmetic  0.6 us (3%)
    pallas_call x1, Pallas kernels, local(): pl.pallas_call(functools.partial(kernel, n, inner, outer, group, head), o...  18.8 us
    convert_element_type x1, other arithmetic, local(): return pl.pallas_call(functools.partial(kernel, n, inner, outer, group, h...  0.6 us

profile of v2, /device:TPU:0, one launch (start us, length us, event | category | flops | bytes accessed | tf_op | source)
XLA Modules:
  0.0 19.4 jit_solution(13260387086355249018)
XLA Ops:
  0.0 18.8 %shard_map.91 = f32[4,512]{1,0:T(4,128)S(1)} custom-call(s32[4,16]{1,0:T(4,128)} %live_hbm.1, s32[4]{0:T(128)} %owner_hbm.1, f32[1,128]{1,0:T(1,128)} %constant.2.clone.freq_hbm, bf16[4,8192]{1,0:T(4,128)(2,1)} %x_hbm.1, bf16[512,1024]{1,0:T(8,128)(2,1)} %wq_hbm.1, bf16[512,256]{1,0:T(8,128)(2,1)} %wkv_hbm.1, bf16[1024,512]{1,0:T(8,128)(2,1)} %wo_hbm.1, ...), custom_call_target="tpu_custom_call" | custom-call | tf_op jit(solution)/shard_map/pallas_call | solution.py:287
  18.8 0.6 %convert_element_type.3 = bf16[4,512]{1,0:T(4,128)(2,1)} convert(f32[4,512]{1,0:T(4,128)S(1)} %shard_map.91) | non-fusion elementwise | flops 2048 | bytes 12288 | tf_op jit(solution)/shard_map/convert_element_type | solution.py:326

commit v3 on v2

--- a/solution.py
+++ b/solution.py
@@ -14,7 +14,7 @@
 BF16 = jnp.bfloat16
 MESH = pl.DeviceIdType.MESH
 CHUNKS = 2
-PARTS = 2
+PARTS = 1
 PIECES = 4
 
 
@@ -73,9 +73,12 @@
             push(src, dst, send, recv, flipped(plane * inner + lax.bitwise_xor(spot, d)))
 
     def over_planes(src, dst, send, recv):
-        for d in [outer // 2] + [d for d in range(1, outer) if d != outer // 2] + [0]:
-            push(src, dst, send, recv, flipped(lax.rem(plane + d, outer) * inner + spot))
-
+        for rank in ranks:
+            push(src, dst, send, recv, flipped(rank * inner + spot))
+
+    up = plane // (outer // 2)
+    ranks = [up * k + (1 - up) * (outer - 1 - k) for k in range(outer)]
+    order = [rank * inner + lax.bitwise_xor(spot, ds) for rank in ranks for ds in range(inner - 1, -1, -1)]
     first = pl.multiple_of(me * rows, rows)
     piece = rows // PIECES
     x_load = pltpu.make_async_copy(x_hbm.at[:, pl.ds(first, rows)], x, load_sem.at[0])
@@ -114,6 +117,8 @@
     for h in range(group):
         part[:, h, :] = projected[:, h * head:(h + 1) * head]
     pl.semaphore_wait(barrier, inner + len(steps))
+    for step in steps:
+        signal(ready.at[2], across(step))
 
     for c in range(CHUNKS):
         in_plane(part.at[pl.ds(c * per, per)], a_in.at[c, spot], send_sem.at[0], a_recv.at[c])
@@ -138,13 +143,13 @@
     sine = jnp.sin(angle)
     sine = jnp.where(lane_id < head // 2, -sine, sine)
 
-    for i in range(max(len(steps) - 1, 1)):
+    k_load.wait()
+    for b in range(batch):
+        keys_t[b] = keys[b, 0].T
+    pl.semaphore_wait(ready.at[2], len(steps))
+    for i in range(1, len(steps) - 1):
         for step in steps:
             signal(ready.at[2 + i], across(step))
-        if i == 0:
-            k_load.wait()
-            for b in range(batch):
-                keys_t[b] = keys[b, 0].T
         pl.semaphore_wait(ready.at[2 + i], len(steps))
     signal(ready.at[0], partner)
     pl.semaphore_wait(ready.at[0], 1)
@@ -171,11 +176,6 @@
     stat_row = lax.broadcasted_iota(jnp.int32, (group, head), 0)
     stat = jnp.zeros((group, head), F32)
     queries = []
-    order = [
-        lax.rem(plane + dz, outer) * inner + lax.bitwise_xor(spot, ds)
-        for ds in sorted(range(inner), key=lambda v: (v % 2 == 0, -v))
-        for dz in sorted(range(outer), key=lambda v: -min(v, outer - v))
-    ]
     scores = []
     for c in range(CHUNKS):
         arrived(b_in.at[c], b_recv.at[c])

time: 19.6 us -> 19.3 us (0.985)
  Pallas kernels: 18.8 us -> 18.6 us
    pallas_call x1, Pallas kernels: 18.8 us -> 18.6 us  [local(): pl.pallas_call(functools.partial(kernel, n, inner, outer, group, head), o...]
where the time goes in v3:
time: 19.3 us; the launch traced here: 19.2 us
  Pallas kernels  18.6 us (96%)
  other arithmetic  0.6 us (3%)
    pallas_call x1, Pallas kernels, local(): pl.pallas_call(functools.partial(kernel, n, inner, outer, group, head), o...  18.6 us
    convert_element_type x1, other arithmetic, local(): return pl.pallas_call(functools.partial(kernel, n, inner, outer, group, h...  0.6 us

profile of v3, /device:TPU:0, one launch (start us, length us, event | category | flops | bytes accessed | tf_op | source)
XLA Modules:
  0.0 19.2 jit_solution(16576283713377678865)
XLA Ops:
  0.0 18.6 %shard_map.91 = f32[4,512]{1,0:T(4,128)S(1)} custom-call(s32[4,16]{1,0:T(4,128)} %live_hbm.1, s32[4]{0:T(128)} %owner_hbm.1, f32[1,128]{1,0:T(1,128)} %constant.2.clone.freq_hbm, bf16[4,8192]{1,0:T(4,128)(2,1)} %x_hbm.1, bf16[512,1024]{1,0:T(8,128)(2,1)} %wq_hbm.1, bf16[512,256]{1,0:T(8,128)(2,1)} %wkv_hbm.1, bf16[1024,512]{1,0:T(8,128)(2,1)} %wo_hbm.1, ...), custom_call_target="tpu_custom_call" | custom-call | tf_op jit(solution)/shard_map/pallas_call | solution.py:287
  18.6 0.6 %convert_element_type.3 = bf16[4,512]{1,0:T(4,128)(2,1)} convert(f32[4,512]{1,0:T(4,128)S(1)} %shard_map.91) | non-fusion elementwise | flops 2048 | bytes 12288 | tf_op jit(solution)/shard_map/convert_element_type | solution.py:326

commit v4 on v3

--- a/solution.py
+++ b/solution.py
@@ -14,7 +14,6 @@
 BF16 = jnp.bfloat16
 MESH = pl.DeviceIdType.MESH
 CHUNKS = 2
-PARTS = 1
 PIECES = 4
 
 
@@ -86,17 +85,15 @@
         pltpu.make_async_copy(wq_hbm.at[pl.ds(i * piece, piece)], wq.at[pl.ds(i * piece, piece)], load_sem.at[1 + i])
         for i in range(PIECES)
     ]
-    later = [(wkv_hbm, wkv), (live_hbm, live), (owner_hbm, owner), (freq_hbm, freq), (k_hbm, keys), (v_hbm, vals)]
-    kv_load, live_load, owner_load, freq_load, k_load, v_load = [
-        pltpu.make_async_copy(src, dst, load_sem.at[1 + PIECES + i]) for i, (src, dst) in enumerate(later)
+    kv_load = pltpu.make_async_copy(wkv_hbm, wkv, load_sem.at[1 + PIECES])
+    later = [(live_hbm, live), (owner_hbm, owner), (freq_hbm, freq), (k_hbm, keys), (v_hbm, vals)]
+    live_load, owner_load, freq_load, k_load, v_load = [
+        pltpu.make_async_copy(src, dst, load_sem.at[i]) for i, (src, dst) in enumerate(later)
     ]
     x_load.start()
     for cp in q_loads:
         cp.start()
     kv_load.start()
-    live_load.start()
-    owner_load.start()
-    freq_load.start()
 
     barrier = pltpu.get_barrier_semaphore()
     signal(barrier, partner)
@@ -106,9 +103,14 @@
         signal(barrier, across(step))
 
     x_load.wait()
+    live_load.start()
     projected = None
     for i, cp in enumerate(q_loads):
         cp.wait()
+        if i == 0:
+            owner_load.start()
+        if i == 1:
+            freq_load.start()
         if i == PIECES - 1:
             k_load.start()
             v_load.start()
@@ -190,26 +192,24 @@
             q = q.astype(BF16)
             queries.append(q)
             scores.append(jnp.dot(q, keys_t[b], preferred_element_type=F32))
-    few = batch // PARTS
-    for c in range(PARTS):
-        accs = []
-        for b in range(c * few, c * few + few):
-            s = jnp.where(slot_id < live[b, me], scores[b] * scaling, -jnp.inf)
-            top = jnp.max(s, -1, keepdims=True)
-            prob = jnp.exp(s - top).astype(BF16)
-            count = jnp.sum(prob.astype(F32), -1, keepdims=True)
-            accs.append(jnp.dot(prob, vals[b, 0], preferred_element_type=F32))
-            stat = jnp.where(stat_lane == b * group + stat_row, top, stat)
-            stat = jnp.where(stat_lane == pairs + b * group + stat_row, count, stat)
-        acc_out[c] = jnp.concatenate(accs, 0).astype(BF16)
-        if c == 0:
-            pl.semaphore_wait(ready.at[1], 1)
-        if c == PARTS - 1:
-            stat_out[...] = jnp.sum(stat, 0, keepdims=True)
-            for j in order:
-                push(stat_out, stat_in.at[me], send_sem.at[0], pair_recv.at[3], flipped(j))
-        for j in order:
-            push(acc_out.at[c], acc_in.at[c, me], send_sem.at[0], g_recv.at[c], flipped(j))
+    accs = []
+    for b in range(batch):
+        s = jnp.where(slot_id < live[b, me], scores[b] * scaling, -jnp.inf)
+        top = jnp.max(s, -1, keepdims=True)
+        prob = jnp.exp(s - top).astype(BF16)
+        count = jnp.sum(prob.astype(F32), -1, keepdims=True)
+        accs.append(jnp.dot(prob, vals[b, 0], preferred_element_type=F32))
+        stat = jnp.where(stat_lane == b * group + stat_row, top, stat)
+        stat = jnp.where(stat_lane == pairs + b * group + stat_row, count, stat)
+    acc_out[...] = jnp.concatenate(accs, 0).astype(BF16)
+    stat_out[...] = jnp.sum(stat, 0, keepdims=True)
+    pl.semaphore_wait(ready.at[1], 1)
+    for side in range(2):
+        peers = order[side * n // 2:(side + 1) * n // 2]
+        for j in peers:
+            push(stat_out, stat_in.at[me], send_sem.at[0], pair_recv.at[3], flipped(j))
+        for j in peers:
+            push(acc_out, acc_in.at[me], send_sem.at[0], g_recv.at[up], flipped(j))
 
     arrived(b_new, b_recv.at[CHUNKS])
     total = b_new[0]
@@ -227,7 +227,9 @@
 
     arrived(stat_in, pair_recv.at[3])
     arrived(new_in, pair_recv.at[1])
-    stats = stat_in[:, 0, :]
+    near = pl.multiple_of(up * (n // 2), n // 2)
+    far = pl.multiple_of((1 - up) * (n // 2), n // 2)
+    stats = jnp.concatenate([stat_in[pl.ds(near, n // 2), 0, :], stat_in[pl.ds(far, n // 2), 0, :]], 0)
     newest = new_in[batch:batch + 1]
     top = jnp.maximum(jnp.max(stats, 0, keepdims=True), newest)
     factor = jnp.exp(stats - top)
@@ -237,17 +239,14 @@
     weight = jnp.where(lane < pairs, factor / whole, 0.0).T
     fresh = jnp.where(lane[:1] < pairs, fresh / whole, 0.0)
     fresh = jnp.broadcast_to(fresh, (group, head)).T
-    for c in range(PARTS):
-        arrived(acc_in.at[c], g_recv.at[c])
-        low_row = c * few * group
-        high_row = low_row + few * group
-        total = weight[low_row:high_row, 0:1] * acc_in[c, 0].astype(F32)
-        for j in range(1, n):
-            total = total + weight[low_row:high_row, j:j + 1] * acc_in[c, j].astype(F32)
-        for i in range(few):
-            b = c * few + i
-            own = fresh[b * group:(b + 1) * group, 0:1] * new_in[b:b + 1]
-            att_rows[b] = total[i * group:(i + 1) * group] + own
+    total = jnp.concatenate([fresh[b * group:(b + 1) * group, 0:1] * new_in[b:b + 1] for b in range(batch)], 0)
+    for side, start in enumerate((near, far)):
+        arrived(acc_in.at[pl.ds(start, n // 2)], g_recv.at[up if side == 0 else 1 - up])
+        for k in range(n // 2):
+            j = side * (n // 2) + k
+            total = total + weight[:pairs, j:j + 1] * acc_in[start + k].astype(F32)
+    for b in range(batch):
+        att_rows[b] = total[b * group:(b + 1) * group]
     attended = jnp.concatenate([att_rows[:, h, :].astype(BF16) for h in range(group)], -1)
 
     arrived(wo, pair_recv.at[0])
@@ -308,16 +307,16 @@
             pltpu.VMEM((2, batch, head), F32),
             pltpu.VMEM((CHUNKS, outer, per, group, head), F32),
             pltpu.VMEM((outer, 2, batch, head), F32),
-            pltpu.VMEM((PARTS, batch // PARTS * group, head), BF16),
-            pltpu.VMEM((PARTS, n, batch // PARTS * group, head), BF16),
+            pltpu.VMEM((batch * group, head), BF16),
+            pltpu.VMEM((n, batch * group, head), BF16),
             pltpu.VMEM((1, head), F32),
             pltpu.VMEM((n, 1, head), F32),
             pltpu.VMEM((batch + 1, head), F32),
             pltpu.VMEM((batch + 1, head), F32),
             pltpu.VMEM((2, batch, cols), F32),
             pltpu.VMEM((batch, group, head), F32),
-            dma((7 + PIECES,)),
-            dma((CHUNKS + 1,)), dma((CHUNKS + 1,)), dma((PARTS,)),
+            dma((2 + PIECES,)),
+            dma((CHUNKS + 1,)), dma((CHUNKS + 1,)), dma((2,)),
             dma((1,)),
             dma((4,)),
             pltpu.SemaphoreType.REGULAR((2 + rounds,)),

time: 19.3 us -> 19.2 us (level)
  Pallas kernels: 18.6 us -> 18.4 us
where the time goes in v4:
time: 19.2 us; the launch traced here: 19.1 us
  Pallas kernels  18.4 us (96%)
  other arithmetic  0.6 us (3%)
    pallas_call x1, Pallas kernels, local(): pl.pallas_call(functools.partial(kernel, n, inner, outer, group, head), o...  18.4 us
    convert_element_type x1, other arithmetic, local(): return pl.pallas_call(functools.partial(kernel, n, inner, outer, group, h...  0.6 us

profile of v4, /device:TPU:0, one launch (start us, length us, event | category | flops | bytes accessed | tf_op | source)
XLA Modules:
  0.0 19.1 jit_solution(810606025429712571)
XLA Ops:
  0.0 18.4 %shard_map.91 = f32[4,512]{1,0:T(4,128)S(1)} custom-call(s32[4,16]{1,0:T(4,128)} %live_hbm.1, s32[4]{0:T(128)} %owner_hbm.1, f32[1,128]{1,0:T(1,128)} %constant.2.clone.freq_hbm, bf16[4,8192]{1,0:T(4,128)(2,1)} %x_hbm.1, bf16[512,1024]{1,0:T(8,128)(2,1)} %wq_hbm.1, bf16[512,256]{1,0:T(8,128)(2,1)} %wkv_hbm.1, bf16[1024,512]{1,0:T(8,128)(2,1)} %wo_hbm.1, ...), custom_call_target="tpu_custom_call" | custom-call | tf_op jit(solution)/shard_map/pallas_call | solution.py:286
  18.5 0.6 %convert_element_type.3 = bf16[4,512]{1,0:T(4,128)(2,1)} convert(f32[4,512]{1,0:T(4,128)S(1)} %shard_map.91) | non-fusion elementwise | flops 2048 | bytes 12288 | tf_op jit(solution)/shard_map/convert_element_type | solution.py:325

commit v5 on v4

--- a/solution.py
+++ b/solution.py
@@ -131,6 +131,7 @@
     part_new[1] = both[:, head:]
     in_plane(part_new, a_new.at[spot], send_sem.at[0], a_recv.at[CHUNKS])
 
+    push(wo_hbm, wo, send_sem.at[0], pair_recv.at[0], partner)
     live_load.wait()
     owner_load.wait()
     freq_load.wait()
@@ -168,8 +169,6 @@
     for j in range(1, inner):
         total = total + a_new[j]
     sum_new[...] = total
-    over_planes(sum_new, b_new.at[plane], send_sem.at[0], b_recv.at[CHUNKS])
-    push(wo_hbm, wo, send_sem.at[0], pair_recv.at[0], partner)
     v_load.wait()
 
     scaling = 1.0 / math.sqrt(head)
@@ -183,6 +182,7 @@
         arrived(b_in.at[c], b_recv.at[c])
         if c == 0:
             signal(ready.at[1], partner)
+            over_planes(sum_new, b_new.at[plane], send_sem.at[0], b_recv.at[CHUNKS])
         total = b_in[c, 0]
         for j in range(1, outer):
             total = total + b_in[c, j]

time: 19.2 us -> 19.1 us (level)
  no operation moved by 1% of the time
where the time goes in v5:
time: 19.1 us; the launch traced here: 18.9 us
  Pallas kernels  18.3 us (96%)
  other arithmetic  0.6 us (3%)
    pallas_call x1, Pallas kernels, local(): pl.pallas_call(functools.partial(kernel, n, inner, outer, group, head), o...  18.3 us
    convert_element_type x1, other arithmetic, local(): return pl.pallas_call(functools.partial(kernel, n, inner, outer, group, h...  0.6 us

profile of v5, /device:TPU:0, one launch (start us, length us, event | category | flops | bytes accessed | tf_op | source)
XLA Modules:
  0.0 18.9 jit_solution(11943304357327837771)
XLA Ops:
  0.0 18.3 %shard_map.91 = f32[4,512]{1,0:T(4,128)S(1)} custom-call(s32[4,16]{1,0:T(4,128)} %live_hbm.1, s32[4]{0:T(128)} %owner_hbm.1, f32[1,128]{1,0:T(1,128)} %constant.2.clone.freq_hbm, bf16[4,8192]{1,0:T(4,128)(2,1)} %x_hbm.1, bf16[512,1024]{1,0:T(8,128)(2,1)} %wq_hbm.1, bf16[512,256]{1,0:T(8,128)(2,1)} %wkv_hbm.1, bf16[1024,512]{1,0:T(8,128)(2,1)} %wo_hbm.1, ...), custom_call_target="tpu_custom_call" | custom-call | tf_op jit(solution)/shard_map/pallas_call | solution.py:286
  18.3 0.6 %convert_element_type.3 = bf16[4,512]{1,0:T(4,128)(2,1)} convert(f32[4,512]{1,0:T(4,128)S(1)} %shard_map.91) | non-fusion elementwise | flops 2048 | bytes 12288 | tf_op jit(solution)/shard_map/convert_element_type | solution.py:325

commit v6 on v5

--- a/solution.py
+++ b/solution.py
@@ -206,7 +206,7 @@
     pl.semaphore_wait(ready.at[1], 1)
     for side in range(2):
         peers = order[side * n // 2:(side + 1) * n // 2]
-        for j in peers:
+        for j in peers[len(peers) // 2:] + peers[:len(peers) // 2]:
             push(stat_out, stat_in.at[me], send_sem.at[0], pair_recv.at[3], flipped(j))
         for j in peers:
             push(acc_out, acc_in.at[me], send_sem.at[0], g_recv.at[up], flipped(j))

time: 19.1 us -> 19.1 us (level)
  no operation moved by 1% of the time
where the time goes in v6:
time: 19.1 us; the launch traced here: 18.9 us
  Pallas kernels  18.3 us (96%)
  other arithmetic  0.6 us (3%)
    pallas_call x1, Pallas kernels, local(): pl.pallas_call(functools.partial(kernel, n, inner, outer, group, head), o...  18.3 us
    convert_element_type x1, other arithmetic, local(): return pl.pallas_call(functools.partial(kernel, n, inner, outer, group, h...  0.6 us

profile of v6, /device:TPU:0, one launch (start us, length us, event | category | flops | bytes accessed | tf_op | source)
XLA Modules:
  0.0 18.9 jit_solution(2553491271414255947)
XLA Ops:
  0.0 18.3 %shard_map.91 = f32[4,512]{1,0:T(4,128)S(1)} custom-call(s32[4,16]{1,0:T(4,128)} %live_hbm.1, s32[4]{0:T(128)} %owner_hbm.1, f32[1,128]{1,0:T(1,128)} %constant.2.clone.freq_hbm, bf16[4,8192]{1,0:T(4,128)(2,1)} %x_hbm.1, bf16[512,1024]{1,0:T(8,128)(2,1)} %wq_hbm.1, bf16[512,256]{1,0:T(8,128)(2,1)} %wkv_hbm.1, bf16[1024,512]{1,0:T(8,128)(2,1)} %wo_hbm.1, ...), custom_call_target="tpu_custom_call" | custom-call | tf_op jit(solution)/shard_map/pallas_call | solution.py:286
  18.3 0.6 %convert_element_type.3 = bf16[4,512]{1,0:T(4,128)(2,1)} convert(f32[4,512]{1,0:T(4,128)S(1)} %shard_map.91) | non-fusion elementwise | flops 2048 | bytes 12288 | tf_op jit(solution)/shard_map/convert_element_type | solution.py:325
